TPU v7x, 32 devices: a whole 2x2x4 slice. The times are simulated.
32 devices in a mesh: rows: 8 (over z, x), leaf: 4 (over y, core).
Axes of the slice: x: 2, y: 2, z: 4, core: 2. Of those that a mesh axis runs over, the one named last changes fastest.
Arguments:
- right_sides: float32 [65536, 128], P(('rows', 'leaf')), may hold values from -30 to 30
- near_blocks: bfloat16 [2, 128, 512, 512], P(None, ('rows', 'leaf')), may hold values from -1 to 2.4
- leaf_bases: bfloat16 [2, 128, 2, 512, 128], P(None, ('rows', 'leaf')), may hold values from -1.5 to 1.5
- local_factors: bfloat16 [2, 224, 3, 128, 128], P(None, ('rows', 'leaf')), may hold values from -1.7 to 1.7
- upper_factors: bfloat16 [2, 32, 3, 3, 128, 128], P(None, ('rows', 'leaf')), may hold values from -1.7 to 1.7, as said below
- top_couplings: bfloat16 [2, 2, 128, 128], replicated, may hold values from -0.5 to 0.5
Outputs:
- solution: float32 [65536, 128], P(('rows', 'leaf'))
- residual_norms: float32 [3, 128], replicated
Inputs may be any that keep to these rules, and one draw needn't show every extreme that they name: upper_factors[s, d, h] is the same for all devices d with the same d // 2 ** (h + 1): the factors of the node h + 1 levels above device d's own node.
All inputs are finite; a program needn't handle non-finite values.
Results may differ from a plain program's by a relative error of at most 0.00095.
Values sent between devices are 32-bit elements; how exact they have to be, the bound alone decides.
A program may use at most 128 MiB of HBM per device.

v0:
```python
import functools
import jax
import jax.numpy as jnp
from jax import lax
from jax.experimental import pallas as pl
from jax.experimental.pallas import tpu as pltpu
from jax.sharding import PartitionSpec as P

STEPS = 3
F32 = jnp.float32
BF16 = jnp.bfloat16
NT = (((1,), (1,)), ((), ()))


def dot(a, b):
    return jnp.dot(a, b, preferred_element_type=F32)


def split(v):
    hi = v.astype(BF16)
    lo = (v - hi.astype(F32)).astype(BF16)
    return hi, lo


def wide(v):
    return jnp.concatenate(split(v), axis=1)


def tall(v):
    return jnp.concatenate(split(v), axis=0)


def fold_cols(v):
    n = v.shape[1] // 2
    return v[:, :n] + v[:, n:]


def fold_rows(v):
    n = v.shape[0] // 2
    return v[:n] + v[n:]


def combine(out):
    n, m = out.shape[0] // 2, out.shape[1] // 2
    return out[:n, :m] + (out[:n, m:] + out[n:, :m])


def group_bits(levels):
    return min(3, levels - 2)


def kernel(
    bits_leaf, bits_rows,
    rhs_hbm, near_hbm, bases_hbm, local_hbm, upper_hbm, top_hbm,
    x_ref, norm_ref,
    b_ref, r_ref, near, bases, local, upper, top,
    vt, pt, tt, et, jt, cb, pre, nrm,
    w_send, w_recv, high_a, high_b, got_a, got_b, plane,
    send_a, send_b, recv_a, recv_b, sib_full, full,
    load_sem, send_sem, recv_sem,
):
    leaves = near.shape[1]
    levels = bits_leaf + bits_rows
    last = levels - 1
    bits = group_bits(levels)
    group = 2**bits
    root = 2 * leaves - 2
    leaf = lax.axis_index("leaf")
    rows = lax.axis_index("rows")
    columns = x_ref.shape[2]
    half = columns // 2
    cut = columns // group
    mine = pl.multiple_of(leaf % 2 * half, half)
    other = pl.multiple_of((1 - leaf % 2) * half, half)
    top_pos = rows // 2 ** (bits_rows - 1)

    def flipped(value, mask):
        for bit in range(mask.bit_length()):
            d = 2**bit
            if mask & d:
                value = value + d - 2 * d * (value // d % 2)
        return value

    def device(mask):
        leaf_mask = mask % 2**bits_leaf
        return (flipped(rows, mask // 2**bits_leaf), flipped(leaf, leaf_mask))

    def member(place):
        row, column = place
        if bits <= bits_leaf:
            return column % group
        return column + 2**bits_leaf * (row % 2 ** (bits - bits_leaf))

    me = member((rows, leaf))
    my_rows = pl.multiple_of(me * cut, cut)

    def load(src, dst, index):
        return pltpu.make_async_copy(src, dst, load_sem.at[index])

    loads = {}
    order = []
    for s in (1, 0):
        order += [
            (("local", s), local_hbm.at[s], local.at[s]),
            (("upper", s), upper_hbm.at[s, 0], upper.at[s]),
            (("bases", s), bases_hbm.at[s], bases.at[s]),
        ]
        if s == 1:
            order += [("res", rhs_hbm, r_ref)]
        order += [
            (("near", s), near_hbm.at[s], near.at[s]),
            (("top", s), top_hbm.at[s], top.at[s]),
        ]
        if s == 1:
            order += [("rhs", rhs_hbm, b_ref)]
    for index, (name, src, dst) in enumerate(order):
        loads[name] = load(src, dst, index)
        loads[name].start()

    barrier = pltpu.get_barrier_semaphore()
    partners = list(range(1, group)) + [2**level for level in range(bits, levels)]
    partners.append(2**last + 2 ** (last - 1))
    for mask in partners:
        pl.semaphore_signal(
            barrier, inc=1, device_id=device(mask), device_id_type=pl.DeviceIdType.MESH
        )

    def chain(s, which):
        product = upper[s, bits - 2, which].astype(F32)
        for index in range(bits - 3, -1, -1):
            product = fold_cols(dot(upper[s, index, which], wide(product)))
        node = {root: fold_cols(dot(local[s, root, which], wide(product)))}
        for n in range(root - 1, -1, -1):
            parent = leaves + n // 2
            node[n] = fold_cols(dot(local[s, n, which], wide(node[parent])))
        return [node[i] for i in range(leaves)]

    def setup_chain(s):
        loads["local", s].wait()
        loads["upper", s].wait()
        et[s] = tall(jnp.concatenate([v.T for v in chain(s, 0)], axis=1))

    def setup_up(s):
        loads["bases", s].wait()
        for i in range(leaves):
            vt[s, i] = bases[s, i, 1].astype(F32).T.astype(BF16)

    def setup_pairs(s):
        for p in range(leaves - 1):
            pair = [local[s, 2 * p + j, 0].astype(F32).T.astype(BF16) for j in range(2)]
            pt[s, p] = jnp.concatenate(pair, axis=1)

    def setup_couplings(s):
        loads["top", s].wait()
        for first, stop in ((1, bits), (bits, levels)):
            product = None
            for level in range(first, stop):
                coupling = top[s, top_pos] if level == last else upper[s, level - 1, 2]
                if product is None:
                    value = coupling.astype(F32)
                else:
                    value = fold_rows(dot(tall(product), coupling))
                tt[s, level] = wide(value.T)
                if level + 1 < stop:
                    q = upper[s, level - 1, 1]
                    product = q.astype(F32) if product is None else fold_rows(dot(tall(product), q))

    def setup_down(s):
        jt[s] = tall(jnp.concatenate(chain(s, 1), axis=0))

    def across(s, value, level):
        return combine(dot(tall(value), tt[s, level]))

    def apply(s, norms, hooks):
        started = []
        counter = [0]

        def start(src, dst, mask):
            index = counter[0]
            counter[0] += 1
            copy = pltpu.make_async_remote_copy(
                src_ref=src,
                dst_ref=dst,
                send_sem=send_sem.at[s, index],
                recv_sem=recv_sem.at[s, index],
                device_id=device(mask),
                device_id_type=pl.DeviceIdType.MESH,
            )
            copy.start()
            started.append(copy)
            return copy

        def pieces(i):
            return wide(x_ref[i]) if s == 0 else r_ref[i].astype(BF16)

        def fold(v):
            return fold_cols(v) if s == 0 else v

        def near_leaf(i):
            value = fold(dot(near[s, i], pieces(i)))
            if s == 0:
                r_ref[i] = b_ref[i] - value
            else:
                x_ref[i] = x_ref[i] + value

        def couple(n):
            sibling = n + 1 - 2 * (n % 2)
            pre[n] = fold_cols(dot(local[s, n, 2], cb[sibling]))

        field = {}

        def inner():
            for p in range(leaves - 1):
                stacked = jnp.concatenate([cb[2 * p], cb[2 * p + 1]], axis=0)
                coefficient = fold_cols(dot(pt[s, p], stacked))
                if p < leaves - 2:
                    cb[leaves + p] = wide(coefficient)
            full[s] = fold_rows(dot(tall(coefficient.T), local[s, root, 0]))
            sib_full[s, 0] = coefficient
            copy_a = start(full.at[s, pl.ds(other, half)], recv_a.at[s, 0], 1)
            copies_b = [start(sib_full.at[s, 0], sib_full.at[s, 1], 1)]
            yield
            for level in range(1, bits):
                copy_a.wait_recv()
                if level == 1:
                    value = full[s, pl.ds(mine, half)] + recv_a[s, 0]
                else:
                    value = send_a[s, level - 1] + recv_a[s, level - 1]
                if level < bits - 1:
                    send_a[s, level] = fold_rows(dot(tall(value), upper[s, level - 1, 0]))
                    copy_a = start(send_a.at[s, level], recv_a.at[s, level], 2**level)
                send_b[s, level] = value
                copies_b.append(start(send_b.at[s, level], recv_b.at[s, level], 2**level))
                if level == 1:
                    for n in range(root):
                        couple(n)
                    copies_b[0].wait_recv()
                    root_pre = fold_cols(dot(local[s, root, 2], wide(sib_full[s, 1])))
                yield
            far = None
            for level in range(1, bits):
                copies_b[level].wait_recv()
                term = across(s, recv_b[s, level], level)
                far = term if far is None else far + term
            sib_full[s, 2, pl.ds(mine, half)] = far
            copy = start(
                sib_full.at[s, 2, pl.ds(mine, half)], sib_full.at[s, 2, pl.ds(mine, half)], 1
            )
            yield
            copy.wait_recv()
            far_t = tall(sib_full[s, 2])
            product = lax.dot_general(local[s, root, 1], far_t, NT, preferred_element_type=F32)
            field[root] = fold_cols(product) + root_pre
            for n in range(root - 1, -1, -1):
                parent = leaves + n // 2
                field[n] = fold_cols(dot(local[s, n, 1], wide(field[parent]))) + pre[n]
            yield

        for i in range(leaves):
            cb[i] = wide(fold(dot(vt[s, i], pieces(i))))
        stacked = jnp.concatenate([cb[i] for i in range(leaves)], axis=0)
        outer_t = combine(dot(et[s], stacked)).T
        size = cut if norms is None else cut + 8
        for j in range(group):
            w_send[s, j, :cut] = outer_t[j * cut : (j + 1) * cut]
            if norms is not None:
                w_send[s, j, cut:] = nrm[0]
        copies_w = []
        for e in range(group - 1, 0, -1):
            copies_w.append(
                start(
                    w_send.at[s, member(device(e)), pl.ds(0, size)],
                    w_recv.at[s, e, pl.ds(0, size)],
                    e,
                )
            )
        steps = inner()
        work = list(range(leaves))
        hooks = list(hooks)

        def fill(everything=False):
            if hooks:
                hooks.pop(0)()
            next(steps, None)
            while work:
                near_leaf(work.pop(0))
                if not everything:
                    break

        fill()
        fill()
        for copy in copies_w:
            copy.wait_recv()
        value = w_send[s, me, pl.ds(0, size)]
        for e in range(1, group):
            value = value + w_recv[s, e, pl.ds(0, size)]
        far = None
        for level in range(bits, last - 1):
            coefficient = value[:cut]
            high_a[s, level, :cut] = fold_rows(dot(tall(coefficient), upper[s, level - 1, 0]))
            if norms is not None:
                high_a[s, level, cut:] = value[cut:]
            copy_a = start(
                high_a.at[s, level, pl.ds(0, size)], got_a.at[s, level, pl.ds(0, size)], 2**level
            )
            high_b[s, level] = coefficient
            copy_b = start(high_b.at[s, level], got_b.at[s, level], 2**level)
            fill()
            copy_a.wait_recv()
            value = high_a[s, level, pl.ds(0, size)] + got_a[s, level, pl.ds(0, size)]
            copy_b.wait_recv()
            term = across(s, got_b[s, level], level)
            far = term if far is None else far + term
        low, high = last - 1, last
        coefficient = value[:cut]
        high_a[s, high, :cut] = fold_rows(dot(tall(coefficient), upper[s, low - 1, 0]))
        high_a[s, low, :cut] = coefficient
        if norms is not None:
            high_a[s, high, cut:] = value[cut:]
            high_a[s, low, cut:] = value[cut:]
        copies_top = [
            start(high_a.at[s, src, pl.ds(0, size)], got_a.at[s, dst, pl.ds(0, size)], mask)
            for src, dst, mask in (
                (high, high + 1, 2**high + 2**low),
                (high, high, 2**high),
                (low, low, 2**low),
            )
        ]
        fill()
        copies_top[2].wait_recv()
        got = got_a[s, low, pl.ds(0, size)]
        if norms is not None:
            value = value + got
        term = across(s, got[:cut], low)
        far = term if far is None else far + term
        fill(True)
        while hooks:
            hooks.pop(0)()
        copies_top[1].wait_recv()
        copies_top[0].wait_recv()
        got = got_a[s, high, pl.ds(0, size)] + got_a[s, high + 1, pl.ds(0, size)]
        if norms is not None:
            nrm[norms] = value[cut:] + got[cut:]
        far = far + across(s, got[:cut], high)
        plane[s, pl.ds(my_rows, cut)] = far
        copies_f = []
        for e in range(group - 1, 0, -1):
            piece = plane.at[s, pl.ds(my_rows, cut)]
            copies_f.append(start(piece, piece, e))
        for _ in steps:
            pass
        for copy in copies_f:
            copy.wait_recv()
        outer = combine(
            lax.dot_general(jt[s], tall(plane[s]), NT, preferred_element_type=F32)
        )
        rank = plane.shape[2]
        partial = None
        for i in range(leaves):
            total = field[i] + outer[i * rank : (i + 1) * rank]
            if s == 0:
                out = r_ref[i] - fold_cols(dot(bases[s, i, 0], wide(total)))
                r_ref[i] = out
                square = jnp.sum((out * out).reshape(-1, 8, out.shape[1]), axis=0)
                partial = square if partial is None else partial + square
            else:
                x_ref[i] = x_ref[i] + dot(bases[s, i, 0], total.astype(BF16))
        if s == 0:
            nrm[0] = partial
        for copy in started:
            copy.wait_send()

    setup_chain(1)
    setup_up(1)
    x_ref[...] = jnp.zeros(x_ref.shape, F32)
    loads["res"].wait()
    pl.semaphore_wait(barrier, len(partners))

    def first():
        setup_pairs(1)
        loads["near", 1].wait()

    def second():
        setup_couplings(1)
        setup_down(1)

    def third():
        setup_chain(0)
        setup_up(0)
        setup_pairs(0)

    def fourth():
        setup_couplings(0)
        setup_down(0)
        loads["near", 0].wait()
        loads["rhs"].wait()

    apply(1, None, [first, second, third, fourth])

    def step(k, carry):
        apply(0, None, [])
        apply(1, k + 1, [])
        return carry

    lax.fori_loop(0, STEPS, step, 0)
    for k in range(STEPS):
        norm_ref[pl.ds(k, 1)] = jnp.sum(nrm[k + 1], axis=0, keepdims=True)


def body(right_sides, near_blocks, leaf_bases, local_factors, upper_factors, top_couplings):
    bits_leaf = lax.axis_size("leaf").bit_length() - 1
    bits_rows = lax.axis_size("rows").bit_length() - 1
    levels = bits_leaf + bits_rows
    leaves, size = near_blocks.shape[1], near_blocks.shape[2]
    rank = leaf_bases.shape[4]
    columns = right_sides.shape[1]
    half = columns // 2
    bits = group_bits(levels)
    group = 2**bits
    cut = columns // group
    copies = 2 * (group - 1) + 2 * levels
    nodes = local_factors.shape[1]
    heights = upper_factors.shape[2]
    vmem = pltpu.VMEM
    out, norms = pl.pallas_call(
        functools.partial(kernel, bits_leaf, bits_rows),
        out_shape=(
            jax.ShapeDtypeStruct((leaves, size, columns), F32),
            jax.ShapeDtypeStruct((STEPS, columns), F32),
        ),
        in_specs=[pl.BlockSpec(memory_space=pl.ANY)] * 6,
        out_specs=(pl.BlockSpec(memory_space=vmem), pl.BlockSpec(memory_space=vmem)),
        scratch_shapes=[
            vmem((leaves, size, columns), F32),
            vmem((leaves, size, columns), F32),
            vmem((2, leaves, size, size), BF16),
            vmem((2, leaves, 2, size, rank), BF16),
            vmem((2, nodes, 3, rank, rank), BF16),
            vmem((2, heights, 3, rank, rank), BF16),
            vmem((2, 2, rank, rank), BF16),
            vmem((2, leaves, rank, size), BF16),
            vmem((2, leaves - 1, rank, 2 * rank), BF16),
            vmem((2, levels, rank, 2 * rank), BF16),
            vmem((2, 2 * rank, leaves * rank), BF16),
            vmem((2, 2 * leaves * rank, rank), BF16),
            vmem((nodes - 1, rank, 2 * columns), BF16),
            vmem((nodes - 1, rank, columns), F32),
            vmem((STEPS + 1, 8, columns), F32),
            vmem((2, group, cut + 8, rank), F32),
            vmem((2, group, cut + 8, rank), F32),
            vmem((2, levels, cut + 8, rank), F32),
            vmem((2, levels, cut, rank), F32),
            vmem((2, levels + 1, cut + 8, rank), F32),
            vmem((2, levels, cut, rank), F32),
            vmem((2, columns, rank), F32),
            vmem((2, bits, half, rank), F32),
            vmem((2, bits, half, rank), F32),
            vmem((2, bits, half, rank), F32),
            vmem((2, bits, half, rank), F32),
            vmem((2, 3, rank, columns), F32),
            vmem((2, columns, rank), F32),
            pltpu.SemaphoreType.DMA((12,)),
            pltpu.SemaphoreType.DMA((2, copies)),
            pltpu.SemaphoreType.DMA((2, copies)),
        ],
        compiler_params=pltpu.CompilerParams(
            collective_id=0, has_side_effects=True, vmem_limit_bytes=67043328
        ),
    )(
        right_sides.reshape(leaves, size, columns),
        near_blocks,
        leaf_bases,
        local_factors,
        upper_factors,
        top_couplings,
    )
    return out.reshape(-1, columns), norms


def solution(mesh):
    placed = (
        P(("rows", "leaf"), None),
        P(None, ("rows", "leaf"), None, None),
        P(None, ("rows", "leaf"), None, None, None),
        P(None, ("rows", "leaf"), None, None, None),
        P(None, ("rows", "leaf"), None, None, None, None),
        P(),
    )
    return jax.shard_map(
        body,
        mesh=mesh,
        in_specs=placed,
        out_specs=(P(("rows", "leaf"), None), P()),
        check_vma=False,
    )
```

profile of v0, /device:TPU:0, one launch (start us, length us, event | category | flops | bytes accessed | tf_op | source)
XLA Modules:
  0.0 100.1 jit_solution(15846794920865278780)
XLA Ops:
  0.6 96.6 %shard_map.77 = (f32[4,512,128]{2,1,0:T(8,128)}, f32[3,128]{1,0:T(4,128)}) custom-call(f32[4,512,128]{2,1,0:T(8,128)} %bitcast.2, bf16[2,4,512,512]{3,2,1,0:T(8,128)(2,1)} %near_hbm.1, bf16[2,4,2,512,128]{4,3,2,1,0:T(8,128)(2,1)} %bases_hbm.1, bf16[2,7,3,128,128]{4,3,2,1,0:T(8,128)(2,1)} %local_hbm.1, bf16[2,1,3,3,128,128]{5,4,3,2,1,0:T(8,128)(2,1)} %upper_hbm.1, ...), custom_call_target="tpu_custom_call" | custom-call | tf_op jit(solution)/shard_map/pallas_call | solution.py:425
  97.3 0.0 copy-start
  97.3 2.3 %copy.10 = f32[2048,128]{1,0:T(8,128)} copy(f32[2048,128]{1,0:T(8,128)} %bitcast.3) | data formatting | bytes 2097152
  99.5 0.0 copy-done
  99.5 0.6 copy.11
Async XLA Ops:
  97.3 2.3 %copy-start = (f32[3,128]{1,0:T(4,128)S(1)}, f32[3,128]{1,0:T(4,128)}, u32[]{:S(2)}) copy-start(f32[3,128]{1,0:T(4,128)} %get-tuple-element.9) | copy-start | bytes 4612
where the time goes:
time: 100 us
  Pallas kernels  96.6 us (97%)
  local copies, waits for them, and re-layouts  2.84 us (3%)
    pallas_call x1, Pallas kernels, body(): pl.pallas_call(functools.partial(kernel, bits_leaf, bits_rows), out_shape...  96.6 us
    unnamed x4, local copies, waits for them, and re-layouts  2.84 us

commit v1 on v0

v1 whole, which is shorter than its diff:
```python
import functools
import jax
import jax.numpy as jnp
from jax import lax
from jax.experimental import pallas as pl
from jax.experimental.pallas import tpu as pltpu
from jax.sharding import PartitionSpec as P

STEPS = 3
F32 = jnp.float32
BF16 = jnp.bfloat16
NT = (((1,), (1,)), ((), ()))


def dot(a, b):
    return jnp.dot(a, b, preferred_element_type=F32)


def split(v):
    hi = v.astype(BF16)
    lo = (v - hi.astype(F32)).astype(BF16)
    return hi, lo


def wide(v):
    return jnp.concatenate(split(v), axis=1)


def tall(v):
    return jnp.concatenate(split(v), axis=0)


def fold_cols(v):
    n = v.shape[1] // 2
    return v[:, :n] + v[:, n:]


def fold_rows(v):
    n = v.shape[0] // 2
    return v[:n] + v[n:]


def combine(out):
    n, m = out.shape[0] // 2, out.shape[1] // 2
    return out[:n, :m] + (out[:n, m:] + out[n:, :m])


def mm(a, b):
    return combine(dot(tall(a), wide(b)))


def dot_nt(a, b):
    return lax.dot_general(a, b, NT, preferred_element_type=F32)


def rows_of(parts):
    return jnp.concatenate(parts, axis=0)


def lanes_of(parts):
    return jnp.concatenate(parts, axis=1)


def norm_rounds(levels):
    return [(lo, min(lo + 5, levels)) for lo in range(0, levels, 5)]


def group_bits(levels):
    return min(3, levels - 2)


def kernel(
    bits_leaf, bits_rows,
    rhs_hbm, near_hbm, bases_hbm, local_hbm, upper_hbm, top_hbm,
    x_ref, norm_ref,
    b_ref, r_ref, near, bases, local, upper, top,
    vt, pt, tt, et, jt, cb, pre, nrm,
    w_send, w_recv, high_a, got_a, plane,
    send_a, send_b, recv_a, recv_b, sib_full, full,
    fac_send, fac_recv, resp_send, resp_recv,
    up_mat, down_mat, side_mat,
    chains, near_coef, rhs_coef, tree, stack,
    out_a, out_b, in_a, in_b, lift, cross, enter,
    fall_a, fall_b, leaf_a, leaf_b, xw, rb, field_a, field_b,
    jw_send, jw_recv, jhigh, jgot, jplane,
    js_a, js_b, jr_a, jr_b, jsib, jfull,
    nsend, nrecv,
    load_sem, send_sem, recv_sem, jsend_sem, jrecv_sem, fsend_sem, frecv_sem, nsend_sem, nrecv_sem,
):
    leaves = near.shape[1]
    levels = bits_leaf + bits_rows
    last = levels - 1
    bits = group_bits(levels)
    group = 2**bits
    root = 2 * leaves - 2
    leaf = lax.axis_index("leaf")
    rows = lax.axis_index("rows")
    columns = x_ref.shape[2]
    rank = plane.shape[1]
    half = columns // 2
    cut = columns // group
    mine = pl.multiple_of(leaf % 2 * half, half)
    other = pl.multiple_of((1 - leaf % 2) * half, half)
    top_pos = rows // 2 ** (bits_rows - 1)

    def flipped(value, mask):
        for bit in range(mask.bit_length()):
            d = 2**bit
            if mask & d:
                value = value + d - 2 * d * (value // d % 2)
        return value

    def device(mask):
        leaf_mask = mask % 2**bits_leaf
        return (flipped(rows, mask // 2**bits_leaf), flipped(leaf, leaf_mask))

    def member(place):
        row, column = place
        if bits <= bits_leaf:
            return column % group
        return column + 2**bits_leaf * (row % 2 ** (bits - bits_leaf))

    me = member((rows, leaf))
    my_rows = pl.multiple_of(me * cut, cut)

    def load(src, dst, index):
        return pltpu.make_async_copy(src, dst, load_sem.at[index])

    loads = {}
    order = []
    for s in (1, 0):
        order += [
            (("local", s), local_hbm.at[s], local.at[s]),
            (("upper", s), upper_hbm.at[s, 0], upper.at[s]),
            (("bases", s), bases_hbm.at[s], bases.at[s]),
        ]
        if s == 1:
            order += [("res", rhs_hbm, r_ref)]
        order += [
            (("near", s), near_hbm.at[s], near.at[s]),
            (("top", s), top_hbm.at[s], top.at[s]),
        ]
        if s == 1:
            order += [("rhs", rhs_hbm, b_ref)]
    for index, (name, src, dst) in enumerate(order):
        loads[name] = load(src, dst, index)
        loads[name].start()

    barrier = pltpu.get_barrier_semaphore()
    partners = set(range(1, group)) | {2**level for level in range(levels)}
    partners.add(2**last + 2 ** (last - 1))
    for lo, hi in norm_rounds(levels):
        partners |= {m << lo for m in range(1, 2 ** (hi - lo))}
    partners = sorted(partners)
    for mask in partners:
        pl.semaphore_signal(
            barrier, inc=1, device_id=device(mask), device_id_type=pl.DeviceIdType.MESH
        )

    def remote(src, dst, sends, recvs, index, mask, started):
        copy = pltpu.make_async_remote_copy(
            src_ref=src,
            dst_ref=dst,
            send_sem=sends.at[index],
            recv_sem=recvs.at[index],
            device_id=device(mask),
            device_id_type=pl.DeviceIdType.MESH,
        )
        copy.start()
        started.append(copy)
        return copy

    def block(i, n=1):
        return pl.ds(i * rank, n * rank)

    def factor(s, level, which):
        return local[s, root, which] if level == 0 else upper[s, level - 1, which]


    def chain(s, which):
        product = upper[s, bits - 2, which].astype(F32)
        for index in range(bits - 3, -1, -1):
            product = fold_cols(dot(upper[s, index, which], wide(product)))
        node = {root: fold_cols(dot(local[s, root, which], wide(product)))}
        for n in range(root - 1, -1, -1):
            parent = leaves + n // 2
            node[n] = fold_cols(dot(local[s, n, which], wide(node[parent])))
        return [node[i] for i in range(leaves)]

    def setup_chain(s):
        loads["local", s].wait()
        loads["upper", s].wait()
        et[...] = tall(lanes_of([v.T for v in chain(s, 0)]))

    def setup_up(s):
        loads["bases", s].wait()
        for i in range(leaves):
            vt[s, i] = bases[s, i, 1].astype(F32).T.astype(BF16)

    def setup_pairs(s):
        for p in range(leaves - 1):
            pair = [local[s, 2 * p + j, 0].astype(F32).T.astype(BF16) for j in range(2)]
            pt[p] = lanes_of(pair)

    def setup_couplings(s):
        loads["top", s].wait()
        for first, stop in ((1, bits), (bits, levels)):
            product = None
            for level in range(first, stop):
                coupling = top[s, top_pos] if level == last else upper[s, level - 1, 2]
                if product is None:
                    value = coupling.astype(F32)
                else:
                    value = fold_rows(dot(tall(product), coupling))
                tt[level] = wide(value.T)
                if level + 1 < stop:
                    q = upper[s, level - 1, 1]
                    product = q.astype(F32) if product is None else fold_rows(dot(tall(product), q))

    def setup_down(s):
        jt[...] = tall(rows_of(chain(s, 1)))

    def apply_first(hooks):
        s = 1
        started = []
        hooks = list(hooks)

        def start(src, dst, mask):
            return remote(src, dst, send_sem, recv_sem, len(started), mask, started)

        def across(value, level):
            return combine(dot(tall(value), tt[level]))

        def near_leaf(i):
            x_ref[i] = dot(near[s, i], r_ref[i].astype(BF16))

        def couple(n):
            sibling = n + 1 - 2 * (n % 2)
            pre[n] = fold_cols(dot(local[s, n, 2], cb[sibling]))

        field = {}

        def inner():
            for p in range(leaves - 1):
                stacked = rows_of([cb[2 * p], cb[2 * p + 1]])
                coefficient = fold_cols(dot(pt[p], stacked))
                if p < leaves - 2:
                    cb[leaves + p] = wide(coefficient)
            full[...] = fold_rows(dot(tall(coefficient.T), local[s, root, 0]))
            sib_full[0] = coefficient
            copy_a = start(full.at[pl.ds(other, half)], recv_a.at[0], 1)
            copies_b = [start(sib_full.at[0], sib_full.at[1], 1)]
            yield
            for level in range(1, bits):
                copy_a.wait_recv()
                if level == 1:
                    value = full[pl.ds(mine, half)] + recv_a[0]
                else:
                    value = send_a[level - 1] + recv_a[level - 1]
                if level < bits - 1:
                    send_a[level] = fold_rows(dot(tall(value), upper[s, level - 1, 0]))
                    copy_a = start(send_a.at[level], recv_a.at[level], 2**level)
                send_b[level] = value
                copies_b.append(start(send_b.at[level], recv_b.at[level], 2**level))
                if level == 1:
                    for n in range(root):
                        couple(n)
                    copies_b[0].wait_recv()
                    root_pre = fold_cols(dot(local[s, root, 2], wide(sib_full[1])))
                yield
            far = None
            for level in range(1, bits):
                copies_b[level].wait_recv()
                term = across(recv_b[level], level)
                far = term if far is None else far + term
            sib_full[2, pl.ds(mine, half)] = far
            piece = sib_full.at[2, pl.ds(mine, half)]
            copy = start(piece, piece, 1)
            yield
            copy.wait_recv()
            product = dot_nt(local[s, root, 1], tall(sib_full[2]))
            field[root] = fold_cols(product) + root_pre
            for n in range(root - 1, -1, -1):
                parent = leaves + n // 2
                field[n] = fold_cols(dot(local[s, n, 1], wide(field[parent]))) + pre[n]
            yield

        for i in range(leaves):
            cb[i] = wide(dot(vt[s, i], r_ref[i].astype(BF16)))
        stacked = rows_of([cb[i] for i in range(leaves)])
        outer_t = combine(dot(et[...], stacked)).T
        for j in range(group):
            w_send[j] = outer_t[j * cut : (j + 1) * cut]
        copies_w = []
        for e in range(group - 1, 0, -1):
            copies_w.append(start(w_send.at[member(device(e))], w_recv.at[e], e))
        steps = inner()
        work = list(range(leaves))

        def fill(everything=False):
            if hooks:
                hooks.pop(0)()
            next(steps, None)
            while work:
                near_leaf(work.pop(0))
                if not everything:
                    break

        fill()
        fill()
        for copy in copies_w:
            copy.wait_recv()
        value = w_send[me]
        for e in range(1, group):
            value = value + w_recv[e]
        far = None
        for level in range(bits, last - 1):
            high_a[level] = fold_rows(dot(tall(value), upper[s, level - 1, 0]))
            high_a[levels + level] = value
            copy_a = start(high_a.at[level], got_a.at[level], 2**level)
            copy_b = start(high_a.at[levels + level], got_a.at[levels + 1 + level], 2**level)
            fill()
            copy_a.wait_recv()
            value = high_a[level] + got_a[level]
            copy_b.wait_recv()
            term = across(got_a[levels + 1 + level], level)
            far = term if far is None else far + term
        low, high = last - 1, last
        high_a[high] = fold_rows(dot(tall(value), upper[s, low - 1, 0]))
        high_a[low] = value
        copies_top = [
            start(high_a.at[src], got_a.at[dst], mask)
            for src, dst, mask in (
                (high, high + 1, 2**high + 2**low),
                (high, high, 2**high),
                (low, low, 2**low),
            )
        ]
        fill()
        copies_top[2].wait_recv()
        term = across(got_a[low], low)
        far = term if far is None else far + term
        fill(True)
        copies_top[1].wait_recv()
        copies_top[0].wait_recv()
        far = far + across(got_a[high] + got_a[high + 1], high)
        plane[pl.ds(my_rows, cut)] = far
        copies_f = []
        for e in range(group - 1, 0, -1):
            piece = plane.at[pl.ds(my_rows, cut)]
            copies_f.append(start(piece, piece, e))
        for _ in steps:
            pass
        while hooks:
            hooks.pop(0)()
        for copy in copies_f:
            copy.wait_recv()
        outer = combine(dot_nt(jt[...], tall(plane[...])))
        for i in range(leaves):
            total = field[i] + outer[i * rank : (i + 1) * rank]
            value = x_ref[i] + dot(bases[s, i, 0], total.astype(BF16))
            x_ref[i] = value
            xw[i] = wide(value)
        for copy in started:
            copy.wait_send()


    pending = []
    replies = {}

    def local_chain(s, which):
        node = {}
        for n in range(root - 1, -1, -1):
            parent = leaves + n // 2
            own = local[s, n, which]
            if parent == root:
                node[n] = own.astype(F32)
            else:
                node[n] = fold_cols(dot(own, wide(node[parent])))
        return rows_of([node[i] for i in range(leaves)])

    def product_vu(i):
        return dot(vt[1, i], bases[0, i, 0])

    def send_response(level, value):
        resp_send[level] = value
        replies["response", level] = remote(
            resp_send.at[level], resp_recv.at[level], fsend_sem, frecv_sem,
            levels + level, 2**level, pending,
        )

    def setup_response():
        loads["local", 0].wait()
        loads["upper", 0].wait()
        for level in range(last):
            fac_send[level] = lanes_of(
                [
                    factor(1, level, 0).astype(F32).T,
                    factor(0, level, 1).astype(F32),
                    factor(0, level, 2).astype(F32),
                ]
            )
            replies["factor", level] = remote(
                fac_send.at[level], fac_recv.at[level], fsend_sem, frecv_sem,
                level, 2**level, pending,
            )
        setup_up(0)
        for s in range(2):
            for which in range(2):
                chains[s, which] = local_chain(s, which)
        middle = rows_of([mm(product_vu(i), chains[0, 1, block(i)]) for i in range(leaves)])
        send_response(0, -mm(chains[1, 0].T, middle))

    def pack(level, x, y, d, c0, c1):
        zero = jnp.zeros((rank, rank), F32)
        if x is not None:
            p = [factor(s, level, 0).astype(F32) for s in range(2)]
            q = [factor(s, level, 1).astype(F32).T for s in range(2)]
            up_mat[level] = rows_of([lanes_of([p[0], x.T]), lanes_of([zero, p[1]])])
            down_mat[level] = rows_of([lanes_of([q[0], y.T]), lanes_of([zero, q[1]])])
            lift[level] = wide(up_mat[level])
        side_mat[level] = rows_of(
            [lanes_of([c0.astype(F32).T, zero]), lanes_of([zero, c1.astype(F32).T]), lanes_of([zero, d.T])]
        )

    def chain_step(level):
        replies["response", level].wait_recv()
        theirs = resp_recv[level]
        if level == last:
            u = fold_rows(dot(tall(theirs), top[0, 1 - top_pos]))
            c1 = top[1, top_pos]
            pack(level, None, None, fold_cols(dot(c1, wide(u))), top[0, top_pos], c1)
            return
        replies["factor", level].wait_recv()
        up = fac_recv[level, :, :rank].astype(BF16)
        sides = fac_recv[level, :, rank:].astype(BF16)
        mixed = fold_rows(dot(tall(theirs), sides))
        lifted = fold_cols(dot(up, wide(mixed)))
        own = fold_rows(dot(tall(resp_send[level]), factor(0, level, 1)))
        own = fold_cols(dot(factor(1, level, 0).astype(F32).T.astype(BF16), wide(own)))
        send_response(level + 1, own + lifted[:, :rank])
        c1 = factor(1, level, 2)
        crossed = fold_cols(dot(c1, wide(mixed)))
        pack(
            level, lifted[:, rank:], crossed[:, :rank], crossed[:, rank:], factor(0, level, 2), c1
        )

    def setup_cross(first, stop):
        product = None
        for level in range(first, stop):
            value = side_mat[level]
            cross[level] = wide(value if product is None else mm(value, product))
            if level + 1 < stop or first == 1:
                step = down_mat[level]
                product = step if product is None else mm(step, product)
        return product

    def ancestors(i, j):
        while i // 2 != j // 2:
            i, j = leaves + i // 2, leaves + j // 2
        return i, j

    def partial(s, which, i, stop):
        value = local[s, i, which].astype(F32)
        n = leaves + i // 2
        while n != stop:
            value = fold_rows(dot(tall(value), local[s, n, which]))
            n = leaves + n // 2
        return value

    def setup_tree(s):
        size = leaves * rank
        tree[s] = jnp.zeros((2 * size, size), BF16)
        for i in range(leaves):
            for j in range(leaves):
                if i == j:
                    continue
                ni, nj = ancestors(i, j)
                if ni == i:
                    tree[s, block(i), block(j)] = local[s, i, 2]
                    continue
                down = fold_rows(dot(tall(partial(s, 1, i, ni)), local[s, ni, 2]))
                value = combine(dot_nt(tall(down), tall(partial(s, 0, j, nj))))
                hi, lo = split(value)
                tree[s, block(i), block(j)] = hi
                tree[s, pl.ds(size + i * rank, rank), block(j)] = lo

    def setup_near():
        loads["near", 0].wait()
        loads["rhs"].wait()
        for i in range(leaves):
            hi, lo = split(dot(vt[1, i], near[0, i]))
            near_coef[i] = rows_of([vt[0, i], hi, lo])
            rhs_coef[block(i)] = fold_cols(dot(vt[1, i], wide(b_ref[i])))

    def setup_plane():
        size = leaves * rank
        inside = tree[0, :size].astype(F32) + tree[0, size:].astype(F32)
        mixed = rows_of([mm(product_vu(i), inside[i * rank : (i + 1) * rank]) for i in range(leaves)])
        up0, up1 = chains[0, 0].T, chains[1, 0].T
        base_a = rows_of([up0, -mm(up1, mixed)])
        p0 = up_mat[0].T
        up = p0
        for level in range(1, bits):
            up = mm(up_mat[level].T, up)
        out_a[...] = tall(mm(up, base_a))
        out_b[...] = tall(mm(up[rank:, rank:], up1))
        in_a[...] = tall(rows_of([base_a, mm(p0, base_a)]))
        in_b[...] = tall(rows_of([up1, mm(p0[rank:, rank:], up1)]))
        down = setup_cross(1, bits)
        enter[...] = wide(rows_of([down_mat[0], side_mat[0]]))
        down = mm(down, down_mat[0])
        leaf_a[...] = tall(chains[0, 1])
        leaf_b[...] = tall(chains[1, 1])
        fall_a[...] = tall(combine(dot_nt(tall(chains[0, 1]), tall(down[:rank, :rank]))))
        fall_b[...] = tall(combine(dot_nt(tall(chains[1, 1]), tall(down[:, rank:]))))


    def merged(k):
        par = k % 2
        started = []

        def start(src, dst, mask):
            return remote(
                src, dst, jsend_sem.at[par], jrecv_sem.at[par], len(started), mask, started
            )

        def across(level, sibling, own):
            value = lanes_of([sibling, own[:, :rank]])
            return combine(dot(tall(value), cross[level]))

        for i in range(leaves):
            out = dot(near_coef[i], xw[i])
            a = fold_cols(out[:rank])
            near_part = out[rank : 2 * rank, :columns] + (
                out[rank : 2 * rank, columns:] + out[2 * rank :, :columns]
            )
            stack[0, block(i)] = wide(a)
            stack[1, block(i)] = wide(rhs_coef[block(i)] - near_part)
        outer = combine(dot(out_a[...], stack[0]))
        outer_b = outer[rank:] + combine(dot(out_b[...], stack[1]))
        outer_t = lanes_of([outer[:rank].T, outer_b.T])
        for j in range(group):
            jw_send[par, j] = outer_t[j * cut : (j + 1) * cut]
        copies_w = []
        for e in range(group - 1, 0, -1):
            copies_w.append(start(jw_send.at[par, member(device(e))], jw_recv.at[par, e], e))

        def inner():
            wide_in = combine(dot(in_a[...], stack[0]))
            narrow = combine(dot(in_b[...], stack[1]))
            jsib[par, 0] = lanes_of([wide_in[:rank].T, (wide_in[rank : 2 * rank] + narrow[:rank]).T])
            jfull[par] = lanes_of(
                [wide_in[2 * rank : 3 * rank].T, (wide_in[3 * rank :] + narrow[rank:]).T]
            )
            copy_a = start(jfull.at[par, pl.ds(other, half)], jr_a.at[par, 0], 1)
            copies_b = [start(jsib.at[par, 0], jsib.at[par, 1], 1)]
            yield
            for level in range(1, bits):
                copy_a.wait_recv()
                if level == 1:
                    value = jfull[par, pl.ds(mine, half)] + jr_a[par, 0]
                else:
                    value = js_a[par, level - 1] + jr_a[par, level - 1]
                if level < bits - 1:
                    js_a[par, level] = combine(dot(tall(value), lift[level]))
                    copy_a = start(js_a.at[par, level], jr_a.at[par, level], 2**level)
                js_b[par, level] = value
                copies_b.append(start(js_b.at[par, level], jr_b.at[par, level], 2**level))
                yield
            far = None
            for level in range(1, bits):
                copies_b[level].wait_recv()
                term = across(level, jr_b[par, level], js_b[par, level])
                far = term if far is None else far + term
            jsib[par, 2, pl.ds(mine, half)] = far
            piece = jsib.at[par, 2, pl.ds(mine, half)]
            copy = start(piece, piece, 1)
            yield
            copies_b[0].wait_recv()
            copy.wait_recv()
            value = lanes_of([jsib[par, 2], jsib[par, 1], jsib[par, 0, :, :rank]])
            value = combine(dot(tall(value), enter[...]))
            field_a[...] = combine(dot_nt(leaf_a[...], tall(value[:, :rank])))
            field_b[...] = combine(dot_nt(leaf_b[...], tall(value[:, rank:])))
            yield

        steps = inner()
        next(steps)
        inside = combine(dot(tree[0], stack[0]))

        def residual(i):
            part = fold_cols(dot(bases[0, i, 0], wide(inside[i * rank : (i + 1) * rank])))
            r_ref[i] = b_ref[i] - fold_cols(dot(near[0, i], xw[i])) - part

        residual(0)
        next(steps)
        for i in range(1, leaves):
            residual(i)
        for copy in copies_w:
            copy.wait_recv()
        value = jw_send[par, me]
        for e in range(1, group):
            value = value + jw_recv[par, e]
        far = None
        for level in range(bits, last - 1):
            jhigh[par, level] = combine(dot(tall(value), lift[level]))
            jhigh[par, levels + level] = value
            copy_a = start(jhigh.at[par, level], jgot.at[par, level], 2**level)
            copy_b = start(
                jhigh.at[par, levels + level], jgot.at[par, levels + 2 + level], 2**level
            )
            copy_a.wait_recv()
            copy_b.wait_recv()
            term = across(level, jgot[par, levels + 2 + level], value)
            far = term if far is None else far + term
            value = jhigh[par, level] + jgot[par, level]
        low, high = last - 1, last
        jhigh[par, high] = combine(dot(tall(value), lift[low]))
        jhigh[par, low] = value
        copies_top = [
            start(jhigh.at[par, src], jgot.at[par, dst], mask)
            for src, dst, mask in (
                (high, high + 1, 2**high + 2**low),
                (high, high, 2**high),
                (high, high + 2, 2**low),
                (low, low, 2**low),
            )
        ]
        for _ in range(bits - 2):
            next(steps)
        copies_top[3].wait_recv()
        term = across(low, jgot[par, low], value)
        far = term if far is None else far + term
        for copy in copies_top[:3]:
            copy.wait_recv()
        own = jhigh[par, high] + jgot[par, high + 2]
        far = far + across(high, jgot[par, high] + jgot[par, high + 1], own)
        jplane[par, pl.ds(my_rows, cut)] = far
        copies_f = []
        for e in range(group - 1, 0, -1):
            piece = jplane.at[par, pl.ds(my_rows, cut)]
            copies_f.append(start(piece, piece, e))
        for _ in steps:
            pass
        for copy in copies_f:
            copy.wait_recv()
        flat = tall(jplane[par])
        alpha = field_a[...] + combine(dot_nt(fall_a[...], flat[:, :rank]))
        sums = None
        for i in range(leaves):
            out = r_ref[i] - fold_cols(dot(bases[0, i, 0], wide(alpha[i * rank : (i + 1) * rank])))
            low_out = out.astype(BF16)
            rb[i] = low_out
            stack[0, block(i)] = wide(dot(vt[1, i], low_out))
            square = jnp.sum((out * out).reshape(-1, 8, columns), axis=0)
            sums = square if sums is None else sums + square
        nrm[pl.ds(k, 1)] = jnp.sum(sums, axis=0, keepdims=True)
        if k == STEPS - 1:
            start_norms()
        beta = field_b[...] + combine(dot_nt(fall_b[...], flat))
        beta = beta + combine(dot(tree[1], stack[0]))
        for i in range(leaves):
            far = beta[i * rank : (i + 1) * rank].astype(BF16)
            value = x_ref[i] + (dot(near[1, i], rb[i]) + dot(bases[1, i, 0], far))
            x_ref[i] = value
            if k < STEPS - 1:
                xw[i] = wide(value)
        for copy in started:
            copy.wait_send()

    norm_copies = []

    def norm_round(index, value):
        lo, hi = norm_rounds(levels)[index]
        nsend[index, pl.ds(0, STEPS)] = value
        copies = []
        for m in range(2 ** (hi - lo) - 1, 0, -1):
            copies.append(
                remote(
                    nsend.at[index, pl.ds(0, STEPS)],
                    nrecv.at[index, m, pl.ds(0, STEPS)],
                    nsend_sem.at[index], nrecv_sem.at[index], m, m << lo, norm_copies,
                )
            )
        return copies

    first_norms = []

    def start_norms():
        first_norms.extend(norm_round(0, nrm[pl.ds(0, STEPS)]))

    def finish_norms():
        copies = first_norms
        for index in range(len(norm_rounds(levels))):
            if index:
                copies = norm_round(index, value)
            for copy in copies:
                copy.wait_recv()
            value = nsend[index, pl.ds(0, STEPS)]
            for m in range(1, len(copies) + 1):
                value = value + nrecv[index, m, pl.ds(0, STEPS)]
        norm_ref[...] = value
        for copy in norm_copies:
            copy.wait_send()

    setup_chain(1)
    setup_up(1)
    loads["res"].wait()
    pl.semaphore_wait(barrier, len(partners))

    def first():
        setup_pairs(1)
        loads["near", 1].wait()
        setup_response()

    def second():
        setup_couplings(1)
        setup_down(1)
        chain_step(0)

    def third():
        loads["top", 0].wait()
        chain_step(1)
        setup_tree(0)

    def fourth():
        setup_tree(1)
        setup_near()

    def fifth():
        for level in range(2, bits):
            chain_step(level)
        setup_plane()

    apply_first([first, second, third, fourth, fifth])
    for level in range(max(2, bits), levels):
        chain_step(level)
    setup_cross(bits, levels)
    for copy in pending:
        copy.wait_send()
    for k in range(STEPS):
        merged(k)
    finish_norms()


def body(right_sides, near_blocks, leaf_bases, local_factors, upper_factors, top_couplings):
    bits_leaf = lax.axis_size("leaf").bit_length() - 1
    bits_rows = lax.axis_size("rows").bit_length() - 1
    levels = bits_leaf + bits_rows
    leaves, size = near_blocks.shape[1], near_blocks.shape[2]
    rank = leaf_bases.shape[4]
    columns = right_sides.shape[1]
    half = columns // 2
    bits = group_bits(levels)
    group = 2**bits
    cut = columns // group
    copies = 2 * (group - 1) + 2 * levels + 4
    nodes = local_factors.shape[1]
    heights = upper_factors.shape[2]
    flat = leaves * rank
    pair = 2 * rank
    rounds = len(norm_rounds(levels))
    vmem = pltpu.VMEM
    dma = pltpu.SemaphoreType.DMA
    out, norms = pl.pallas_call(
        functools.partial(kernel, bits_leaf, bits_rows),
        out_shape=(
            jax.ShapeDtypeStruct((leaves, size, columns), F32),
            jax.ShapeDtypeStruct((STEPS, columns), F32),
        ),
        in_specs=[pl.BlockSpec(memory_space=pl.ANY)] * 6,
        out_specs=(pl.BlockSpec(memory_space=vmem), pl.BlockSpec(memory_space=vmem)),
        scratch_shapes=[
            vmem((leaves, size, columns), F32),
            vmem((leaves, size, columns), F32),
            vmem((2, leaves, size, size), BF16),
            vmem((2, leaves, 2, size, rank), BF16),
            vmem((2, nodes, 3, rank, rank), BF16),
            vmem((2, heights, 3, rank, rank), BF16),
            vmem((2, 2, rank, rank), BF16),
            vmem((2, leaves, rank, size), BF16),
            vmem((leaves - 1, rank, 2 * rank), BF16),
            vmem((levels, rank, 2 * rank), BF16),
            vmem((2 * rank, leaves * rank), BF16),
            vmem((2 * leaves * rank, rank), BF16),
            vmem((nodes - 1, rank, 2 * columns), BF16),
            vmem((nodes - 1, rank, columns), F32),
            vmem((8, columns), F32),
            vmem((group, cut, rank), F32),
            vmem((group, cut, rank), F32),
            vmem((2 * levels, cut, rank), F32),
            vmem((2 * levels + 1, cut, rank), F32),
            vmem((columns, rank), F32),
            vmem((bits, half, rank), F32),
            vmem((bits, half, rank), F32),
            vmem((bits, half, rank), F32),
            vmem((bits, half, rank), F32),
            vmem((3, rank, columns), F32),
            vmem((columns, rank), F32),
            vmem((levels - 1, rank, 3 * rank), F32),
            vmem((levels - 1, rank, 3 * rank), F32),
            vmem((levels, rank, rank), F32),
            vmem((levels, rank, rank), F32),
            vmem((levels, pair, pair), F32),
            vmem((levels, pair, pair), F32),
            vmem((levels, 3 * rank, pair), F32),
            vmem((2, 2, flat, rank), F32),
            vmem((leaves, 3 * rank, size), BF16),
            vmem((flat, columns), F32),
            vmem((2, 2 * flat, flat), BF16),
            vmem((2, flat, 2 * columns), BF16),
            vmem((2 * pair, flat), BF16),
            vmem((pair, flat), BF16),
            vmem((4 * pair, flat), BF16),
            vmem((2 * pair, flat), BF16),
            vmem((levels, pair, 2 * pair), BF16),
            vmem((levels, 3 * rank, 2 * pair), BF16),
            vmem((5 * rank, 2 * pair), BF16),
            vmem((2 * flat, rank), BF16),
            vmem((2 * flat, pair), BF16),
            vmem((2 * flat, rank), BF16),
            vmem((2 * flat, rank), BF16),
            vmem((leaves, size, 2 * columns), BF16),
            vmem((leaves, size, columns), BF16),
            vmem((flat, columns), F32),
            vmem((flat, columns), F32),
            vmem((2, group, cut, pair), F32),
            vmem((2, group, cut, pair), F32),
            vmem((2, 2 * levels, cut, pair), F32),
            vmem((2, 2 * levels + 2, cut, pair), F32),
            vmem((2, columns, pair), F32),
            vmem((2, bits, half, pair), F32),
            vmem((2, bits, half, pair), F32),
            vmem((2, bits, half, pair), F32),
            vmem((2, bits, half, pair), F32),
            vmem((2, 3, columns, pair), F32),
            vmem((2, columns, pair), F32),
            vmem((rounds, 8, columns), F32),
            vmem((rounds, 32, 8, columns), F32),
            dma((12,)),
            dma((copies,)),
            dma((copies,)),
            dma((2, copies)),
            dma((2, copies)),
            dma((2 * levels,)),
            dma((2 * levels,)),
            dma((rounds, 32)),
            dma((rounds, 32)),
        ],
        compiler_params=pltpu.CompilerParams(
            collective_id=0, has_side_effects=True, vmem_limit_bytes=67043328
        ),
    )(
        right_sides.reshape(leaves, size, columns),
        near_blocks,
        leaf_bases,
        local_factors,
        upper_factors,
        top_couplings,
    )
    return out.reshape(-1, columns), norms


def solution(mesh):
    placed = (
        P(("rows", "leaf"), None),
        P(None, ("rows", "leaf"), None, None),
        P(None, ("rows", "leaf"), None, None, None),
        P(None, ("rows", "leaf"), None, None, None),
        P(None, ("rows", "leaf"), None, None, None, None),
        P(),
    )
    return jax.shard_map(
        body,
        mesh=mesh,
        in_specs=placed,
        out_specs=(P(("rows", "leaf"), None), P()),
        check_vma=False,
    )
```

time: 100 us -> 90.4 us (0.904)
  Pallas kernels: 96.6 us -> 86.8 us
    pallas_call x1, Pallas kernels: 96.6 us -> 86.8 us  [body(): pl.pallas_call(functools.partial(kernel, bits_leaf, bits_rows), out_shape...]
where the time goes in v1:
time: 90.4 us; the launch traced here: 90.3 us
  Pallas kernels  86.8 us (96%)
  local copies, waits for them, and re-layouts  2.84 us (3%)
    pallas_call x1, Pallas kernels, body(): pl.pallas_call(functools.partial(kernel, bits_leaf, bits_rows), out_shape...  86.8 us
    unnamed x4, local copies, waits for them, and re-layouts  2.84 us

profile of v1, /device:TPU:0, one launch (start us, length us, event | category | flops | bytes accessed | tf_op | source)
XLA Modules:
  0.0 90.3 jit_solution(18350581265713107343)
XLA Ops:
  0.6 86.8 %shard_map.77 = (f32[4,512,128]{2,1,0:T(8,128)}, f32[3,128]{1,0:T(4,128)}) custom-call(f32[4,512,128]{2,1,0:T(8,128)} %bitcast.2, bf16[2,4,512,512]{3,2,1,0:T(8,128)(2,1)} %near_hbm.1, bf16[2,4,2,512,128]{4,3,2,1,0:T(8,128)(2,1)} %bases_hbm.1, bf16[2,7,3,128,128]{4,3,2,1,0:T(8,128)(2,1)} %local_hbm.1, bf16[2,1,3,3,128,128]{5,4,3,2,1,0:T(8,128)(2,1)} %upper_hbm.1, ...), custom_call_target="tpu_custom_call" | custom-call | tf_op jit(solution)/shard_map/pallas_call | solution.py:766
  87.4 0.0 copy-start
  87.4 2.3 %copy.10 = f32[2048,128]{1,0:T(8,128)} copy(f32[2048,128]{1,0:T(8,128)} %bitcast.3) | data formatting | bytes 2097152
  89.7 0.0 copy-done
  89.7 0.6 copy.11
Async XLA Ops:
  87.4 2.3 %copy-start = (f32[3,128]{1,0:T(4,128)S(1)}, f32[3,128]{1,0:T(4,128)}, u32[]{:S(2)}) copy-start(f32[3,128]{1,0:T(4,128)} %get-tuple-element.9) | copy-start | bytes 4612

commit v2 on v1

--- a/solution.py
+++ b/solution.py
@@ -79,13 +79,14 @@
     send_a, send_b, recv_a, recv_b, sib_full, full,
     fac_send, fac_recv, resp_send, resp_recv,
     up_mat, down_mat, side_mat,
+    gram, base_a, base_b,
     chains, near_coef, rhs_coef, tree, stack,
     out_a, out_b, in_a, in_b, lift, cross, enter,
     fall_a, fall_b, leaf_a, leaf_b, xw, rb, field_a, field_b,
     jw_send, jw_recv, jhigh, jgot, jplane,
     js_a, js_b, jr_a, jr_b, jsib, jfull,
     nsend, nrecv,
-    load_sem, send_sem, recv_sem, jsend_sem, jrecv_sem, fsend_sem, frecv_sem, nsend_sem, nrecv_sem,
+    load_sem, send_sem, recv_sem, fsend_sem, frecv_sem, nsend_sem, nrecv_sem,
 ):
     leaves = near.shape[1]
     levels = bits_leaf + bits_rows
@@ -149,8 +150,6 @@
     barrier = pltpu.get_barrier_semaphore()
     partners = set(range(1, group)) | {2**level for level in range(levels)}
     partners.add(2**last + 2 ** (last - 1))
-    for lo, hi in norm_rounds(levels):
-        partners |= {m << lo for m in range(1, 2 ** (hi - lo))}
     partners = sorted(partners)
     for mask in partners:
         pl.semaphore_signal(
@@ -220,13 +219,13 @@
     def setup_down(s):
         jt[...] = tall(rows_of(chain(s, 1)))
 
-    def apply_first(hooks):
+    def apply_first(prepare, hooks):
         s = 1
         started = []
         hooks = list(hooks)
 
         def start(src, dst, mask):
-            return remote(src, dst, send_sem, recv_sem, len(started), mask, started)
+            return remote(src, dst, send_sem, recv_sem.at[1], len(started), mask, started)
 
         def across(value, level):
             return combine(dot(tall(value), tt[level]))
@@ -291,6 +290,7 @@
         outer_t = combine(dot(et[...], stacked)).T
         for j in range(group):
             w_send[j] = outer_t[j * cut : (j + 1) * cut]
+        prepare()
         copies_w = []
         for e in range(group - 1, 0, -1):
             copies_w.append(start(w_send.at[member(device(e))], w_recv.at[e], e))
@@ -366,6 +366,7 @@
 
 
     pending = []
+    own_part = {}
     replies = {}
 
     def local_chain(s, which):
@@ -379,19 +380,30 @@
                 node[n] = fold_cols(dot(own, wide(node[parent])))
         return rows_of([node[i] for i in range(leaves)])
 
-    def product_vu(i):
-        return dot(vt[1, i], bases[0, i, 0])
-
     def send_response(level, value):
-        resp_send[level] = value
+        if value is not None:
+            resp_send[level] = value
         replies["response", level] = remote(
             resp_send.at[level], resp_recv.at[level], fsend_sem, frecv_sem,
             levels + level, 2**level, pending,
         )
 
-    def setup_response():
+    def lift_response(level):
+        own = fold_rows(dot(tall(resp_send[level]), factor(0, level, 1)))
+        up = fac_send[level, :, :rank].astype(BF16)
+        own_part[level] = fold_cols(dot(up, wide(own)))
+
+    def prepare_response():
         loads["local", 0].wait()
         loads["upper", 0].wait()
+        setup_up(0)
+        for s in range(2):
+            for which in range(2):
+                chains[s, which] = local_chain(s, which)
+        for i in range(leaves):
+            gram[block(i)] = dot(vt[1, i], bases[0, i, 0])
+        middle = rows_of([mm(gram[block(i)], chains[0, 1, block(i)]) for i in range(leaves)])
+        resp_send[0] = -mm(chains[1, 0].T, middle)
         for level in range(last):
             fac_send[level] = lanes_of(
                 [
@@ -400,16 +412,13 @@
                     factor(0, level, 2).astype(F32),
                 ]
             )
+
+    def send_factors(which):
+        for level in which:
             replies["factor", level] = remote(
                 fac_send.at[level], fac_recv.at[level], fsend_sem, frecv_sem,
                 level, 2**level, pending,
             )
-        setup_up(0)
-        for s in range(2):
-            for which in range(2):
-                chains[s, which] = local_chain(s, which)
-        middle = rows_of([mm(product_vu(i), chains[0, 1, block(i)]) for i in range(leaves)])
-        send_response(0, -mm(chains[1, 0].T, middle))
 
     def pack(level, x, y, d, c0, c1):
         zero = jnp.zeros((rank, rank), F32)
@@ -436,9 +445,9 @@
         sides = fac_recv[level, :, rank:].astype(BF16)
         mixed = fold_rows(dot(tall(theirs), sides))
         lifted = fold_cols(dot(up, wide(mixed)))
-        own = fold_rows(dot(tall(resp_send[level]), factor(0, level, 1)))
-        own = fold_cols(dot(factor(1, level, 0).astype(F32).T.astype(BF16), wide(own)))
-        send_response(level + 1, own + lifted[:, :rank])
+        send_response(level + 1, own_part[level] + lifted[:, :rank])
+        if level + 1 < last:
+            lift_response(level + 1)
         c1 = factor(1, level, 2)
         crossed = fold_cols(dot(c1, wide(mixed)))
         pack(
@@ -493,20 +502,27 @@
             near_coef[i] = rows_of([vt[0, i], hi, lo])
             rhs_coef[block(i)] = fold_cols(dot(vt[1, i], wide(b_ref[i])))
 
-    def setup_plane():
+    def setup_base():
         size = leaves * rank
         inside = tree[0, :size].astype(F32) + tree[0, size:].astype(F32)
-        mixed = rows_of([mm(product_vu(i), inside[i * rank : (i + 1) * rank]) for i in range(leaves)])
+        mixed = rows_of([mm(gram[block(i)], inside[i * rank : (i + 1) * rank]) for i in range(leaves)])
         up0, up1 = chains[0, 0].T, chains[1, 0].T
-        base_a = rows_of([up0, -mm(up1, mixed)])
-        p0 = up_mat[0].T
-        up = p0
+        base_a[...] = rows_of([up0, -mm(up1, mixed)])
+        base_b[...] = up1
+
+    def setup_rise():
+        up = up_mat[0].T
         for level in range(1, bits):
             up = mm(up_mat[level].T, up)
-        out_a[...] = tall(mm(up, base_a))
-        out_b[...] = tall(mm(up[rank:, rank:], up1))
-        in_a[...] = tall(rows_of([base_a, mm(p0, base_a)]))
-        in_b[...] = tall(rows_of([up1, mm(p0[rank:, rank:], up1)]))
+        out_a[...] = tall(mm(up, base_a[...]))
+        out_b[...] = tall(mm(up[rank:, rank:], base_b[...]))
+
+    def setup_enter():
+        p0 = up_mat[0].T
+        in_a[...] = tall(rows_of([base_a[...], mm(p0, base_a[...])]))
+        in_b[...] = tall(rows_of([base_b[...], mm(p0[rank:, rank:], base_b[...])]))
+
+    def setup_fall():
         down = setup_cross(1, bits)
         enter[...] = wide(rows_of([down_mat[0], side_mat[0]]))
         down = mm(down, down_mat[0])
@@ -516,13 +532,18 @@
         fall_b[...] = tall(combine(dot_nt(tall(chains[1, 1]), tall(down[:, rank:]))))
 
 
-    def merged(k):
+    def merged(k, hooks):
         par = k % 2
         started = []
+        hooks = list(hooks)
+
+        def hook():
+            if hooks:
+                hooks.pop(0)()
 
         def start(src, dst, mask):
             return remote(
-                src, dst, jsend_sem.at[par], jrecv_sem.at[par], len(started), mask, started
+                src, dst, send_sem, recv_sem.at[par], len(started), mask, started
             )
 
         def across(level, sibling, own):
@@ -545,6 +566,8 @@
         copies_w = []
         for e in range(group - 1, 0, -1):
             copies_w.append(start(jw_send.at[par, member(device(e))], jw_recv.at[par, e], e))
+
+        hook()
 
         def inner():
             wide_in = combine(dot(in_a[...], stack[0]))
@@ -595,6 +618,7 @@
 
         residual(0)
         next(steps)
+        hook()
         for i in range(1, leaves):
             residual(i)
         for copy in copies_w:
@@ -629,6 +653,7 @@
         ]
         for _ in range(bits - 2):
             next(steps)
+        hook()
         copies_top[3].wait_recv()
         term = across(low, jgot[par, low], value)
         far = term if far is None else far + term
@@ -669,78 +694,89 @@
         for copy in started:
             copy.wait_send()
 
-    norm_copies = []
-
     def norm_round(index, value):
         lo, hi = norm_rounds(levels)[index]
         nsend[index, pl.ds(0, STEPS)] = value
-        copies = []
         for m in range(2 ** (hi - lo) - 1, 0, -1):
-            copies.append(
-                remote(
-                    nsend.at[index, pl.ds(0, STEPS)],
-                    nrecv.at[index, m, pl.ds(0, STEPS)],
-                    nsend_sem.at[index], nrecv_sem.at[index], m, m << lo, norm_copies,
-                )
-            )
-        return copies
-
-    first_norms = []
+            pltpu.make_async_remote_copy(
+                src_ref=nsend.at[index, pl.ds(0, STEPS)],
+                dst_ref=nrecv.at[index, m, pl.ds(0, STEPS)],
+                send_sem=nsend_sem.at[index],
+                recv_sem=nrecv_sem.at[index],
+                device_id=device(m << lo),
+                device_id_type=pl.DeviceIdType.MESH,
+            ).start()
 
     def start_norms():
-        first_norms.extend(norm_round(0, nrm[pl.ds(0, STEPS)]))
+        norm_round(0, nrm[pl.ds(0, STEPS)])
 
     def finish_norms():
-        copies = first_norms
-        for index in range(len(norm_rounds(levels))):
+        waits = []
+        for index, (lo, hi) in enumerate(norm_rounds(levels)):
             if index:
-                copies = norm_round(index, value)
-            for copy in copies:
-                copy.wait_recv()
+                norm_round(index, value)
+            count = 2 ** (hi - lo)
+            every = nrecv.at[index, pl.ds(1, count - 1), pl.ds(0, STEPS)]
+            pltpu.make_async_copy(every, every, nrecv_sem.at[index]).wait()
+            waits.append(pltpu.make_async_copy(every, every, nsend_sem.at[index]))
             value = nsend[index, pl.ds(0, STEPS)]
-            for m in range(1, len(copies) + 1):
+            for m in range(1, count):
                 value = value + nrecv[index, m, pl.ds(0, STEPS)]
         norm_ref[...] = value
-        for copy in norm_copies:
-            copy.wait_send()
+        for copy in waits:
+            copy.wait()
 
     setup_chain(1)
     setup_up(1)
     loads["res"].wait()
-    pl.semaphore_wait(barrier, len(partners))
+
+    def prepare():
+        prepare_response()
+        setup_tree(0)
+        pl.semaphore_wait(barrier, len(partners))
 
     def first():
+        send_response(0, None)
+        send_factors([level for level in range(last) if level != 1])
+        lift_response(0)
         setup_pairs(1)
         loads["near", 1].wait()
-        setup_response()
 
     def second():
+        chain_step(0)
         setup_couplings(1)
         setup_down(1)
-        chain_step(0)
 
     def third():
+        send_factors([1])
         loads["top", 0].wait()
+        setup_near()
+
+    def fourth():
         chain_step(1)
-        setup_tree(0)
-
-    def fourth():
-        setup_tree(1)
-        setup_near()
 
     def fifth():
+        setup_base()
         for level in range(2, bits):
             chain_step(level)
-        setup_plane()
-
-    apply_first([first, second, third, fourth, fifth])
-    for level in range(max(2, bits), levels):
-        chain_step(level)
-    setup_cross(bits, levels)
-    for copy in pending:
-        copy.wait_send()
-    for k in range(STEPS):
-        merged(k)
+        setup_rise()
+
+    def sixth():
+        setup_tree(1)
+        for level in range(bits, last):
+            chain_step(level)
+
+    def seventh():
+        setup_fall()
+        chain_step(last)
+        setup_cross(bits, levels)
+        for copy in pending:
+            copy.wait_send()
+
+    apply_first(prepare, [first, second, third, fourth, fifth])
+    merged(0, [setup_enter, sixth, seventh])
+    for k in range(1, STEPS):
+        merged(k, [lambda: None])
     finish_norms()
 
 
@@ -755,7 +791,7 @@
     bits = group_bits(levels)
     group = 2**bits
     cut = columns // group
-    copies = 2 * (group - 1) + 2 * levels + 4
+    copies = 2 * (group - 1) + 2 * bits + 2 * (levels - 2 - bits) + 4
     nodes = local_factors.shape[1]
     heights = upper_factors.shape[2]
     flat = leaves * rank
@@ -766,8 +802,8 @@
     out, norms = pl.pallas_call(
         functools.partial(kernel, bits_leaf, bits_rows),
         out_shape=(
-            jax.ShapeDtypeStruct((leaves, size, columns), F32),
-            jax.ShapeDtypeStruct((STEPS, columns), F32),
+            vmem((leaves, size, columns), F32),
+            vmem((STEPS, columns), F32),
         ),
         in_specs=[pl.BlockSpec(memory_space=pl.ANY)] * 6,
         out_specs=(pl.BlockSpec(memory_space=vmem), pl.BlockSpec(memory_space=vmem)),
@@ -805,6 +841,9 @@
             vmem((levels, pair, pair), F32),
             vmem((levels, pair, pair), F32),
             vmem((levels, 3 * rank, pair), F32),
+            vmem((flat, rank), F32),
+            vmem((pair, flat), F32),
+            vmem((rank, flat), F32),
             vmem((2, 2, flat, rank), F32),
             vmem((leaves, 3 * rank, size), BF16),
             vmem((flat, columns), F32),
@@ -840,16 +879,14 @@
             vmem((rounds, 32, 8, columns), F32),
             dma((12,)),
             dma((copies,)),
-            dma((copies,)),
-            dma((2, copies)),
             dma((2, copies)),
             dma((2 * levels,)),
             dma((2 * levels,)),
-            dma((rounds, 32)),
-            dma((rounds, 32)),
+            dma((rounds,)),
+            dma((rounds,)),
         ],
         compiler_params=pltpu.CompilerParams(
-            collective_id=0, has_side_effects=True, vmem_limit_bytes=67043328
+            collective_id=0, has_side_effects=True, vmem_limit_bytes=60000000
         ),
     )(
         right_sides.reshape(leaves, size, columns),

time: 90.4 us -> 80.8 us (0.89)
  Pallas kernels: 86.8 us -> 78.4 us
  local copies, waits for them, and re-layouts: 2.84 us -> 1.55 us
    pallas_call x1, Pallas kernels: 86.8 us -> 78.4 us  [body(): pl.pallas_call(functools.partial(kernel, bits_leaf, bits_rows), out_shape...]
    unnamed x4 -> x2, local copies, waits for them, and re-layouts: 2.84 us -> 1.55 us
where the time goes in v2:
time: 80.8 us; the launch traced here: 80.6 us
  Pallas kernels  78.4 us (97%)
  local copies, waits for them, and re-layouts  1.55 us (2%)
    pallas_call x1, Pallas kernels, body(): pl.pallas_call(functools.partial(kernel, bits_leaf, bits_rows), out_shape...  78.4 us

profile of v2, /device:TPU:0, one launch (start us, length us, event | category | flops | bytes accessed | tf_op | source)
XLA Modules:
  0.0 80.6 jit_solution(10602758123806955738)
XLA Ops:
  0.6 78.4 %shard_map.77 = (f32[4,512,128]{2,1,0:T(8,128)S(1)}, f32[3,128]{1,0:T(4,128)S(1)}) custom-call(f32[4,512,128]{2,1,0:T(8,128)} %bitcast.3, bf16[2,4,512,512]{3,2,1,0:T(8,128)(2,1)} %near_hbm.1, bf16[2,4,2,512,128]{4,3,2,1,0:T(8,128)(2,1)} %bases_hbm.1, bf16[2,7,3,128,128]{4,3,2,1,0:T(8,128)(2,1)} %local_hbm.1, bf16[2,1,3,3,128,128]{5,4,3,2,1,0:T(8,128)(2,1)} %upper_hbm.1, ...), custom_call_target="tpu_custom_call" | custom-call | tf_op jit(solution)/shard_map/pallas_call | solution.py:802
  79.1 1.0 %copy.10 = f32[2048,128]{1,0:T(8,128)} copy(f32[2048,128]{1,0:T(8,128)S(1)} %bitcast.2) | data formatting | bytes 2097152
  80.1 0.6 copy.11

commit v3 on v2

--- a/solution.py
+++ b/solution.py
@@ -168,6 +168,8 @@
         copy.start()
         started.append(copy)
         return copy
+
+    share = pl.ds(pl.multiple_of(leaf % 2 * (rank // 2), rank // 2), rank // 2)
 
     def block(i, n=1):
         return pl.ds(i * rank, n * rank)
@@ -413,12 +415,20 @@
                 ]
             )
 
-    def send_factors(which):
-        for level in which:
+    def send_factors():
+        for level in range(last):
+            part = pl.ds(0, rank) if level == 0 else share
             replies["factor", level] = remote(
-                fac_send.at[level], fac_recv.at[level], fsend_sem, frecv_sem,
+                fac_send.at[level, part], fac_recv.at[level, part], fsend_sem, frecv_sem,
                 level, 2**level, pending,
             )
+
+    def forward_factor(level):
+        replies["factor", level].wait_recv()
+        piece = fac_recv.at[level, share]
+        replies["factor", level] = remote(
+            piece, piece, fsend_sem, frecv_sem, 2 * levels + level, 1, pending
+        )
 
     def pack(level, x, y, d, c0, c1):
         zero = jnp.zeros((rank, rank), F32)
@@ -737,7 +747,7 @@
 
     def first():
         send_response(0, None)
-        send_factors([level for level in range(last) if level != 1])
+        send_factors()
         lift_response(0)
         setup_pairs(1)
         loads["near", 1].wait()
@@ -748,33 +758,36 @@
         setup_down(1)
 
     def third():
-        send_factors([1])
+        for level in range(1, bits):
+            forward_factor(level)
         loads["top", 0].wait()
         setup_near()
+        chain_step(1)
 
     def fourth():
-        chain_step(1)
+        setup_base()
+        setup_tree(1)
 
     def fifth():
-        setup_base()
+        for level in range(bits, last):
+            forward_factor(level)
         for level in range(2, bits):
             chain_step(level)
         setup_rise()
 
     def sixth():
-        setup_tree(1)
+        setup_enter()
         for level in range(bits, last):
             chain_step(level)
 
-    def seventh():
-        setup_fall()
+    def eighth():
         chain_step(last)
         setup_cross(bits, levels)
         for copy in pending:
             copy.wait_send()
 
     apply_first(prepare, [first, second, third, fourth, fifth])
-    merged(0, [setup_enter, sixth, seventh])
+    merged(0, [sixth, setup_fall, eighth])
     for k in range(1, STEPS):
         merged(k, [lambda: None])
     finish_norms()
@@ -880,8 +893,8 @@
             dma((12,)),
             dma((copies,)),
             dma((2, copies)),
-            dma((2 * levels,)),
-            dma((2 * levels,)),
+            dma((3 * levels,)),
+            dma((3 * levels,)),
             dma((rounds,)),
             dma((rounds,)),
         ],

time: 80.8 us -> 78.9 us (0.976)
  Pallas kernels: 78.4 us -> 76.5 us
    pallas_call x1, Pallas kernels: 78.4 us -> 76.5 us  [body(): pl.pallas_call(functools.partial(kernel, bits_leaf, bits_rows), out_shape...]
where the time goes in v3:
time: 78.9 us; the launch traced here: 78.7 us
  Pallas kernels  76.5 us (97%)
  local copies, waits for them, and re-layouts  1.55 us (2%)
    pallas_call x1, Pallas kernels, body(): pl.pallas_call(functools.partial(kernel, bits_leaf, bits_rows), out_shape...  76.5 us

profile of v3, /device:TPU:0, one launch (start us, length us, event | category | flops | bytes accessed | tf_op | source)
XLA Modules:
  0.0 78.7 jit_solution(9507917361020611746)
XLA Ops:
  0.6 76.5 %shard_map.77 = (f32[4,512,128]{2,1,0:T(8,128)S(1)}, f32[3,128]{1,0:T(4,128)S(1)}) custom-call(f32[4,512,128]{2,1,0:T(8,128)} %bitcast.3, bf16[2,4,512,512]{3,2,1,0:T(8,128)(2,1)} %near_hbm.1, bf16[2,4,2,512,128]{4,3,2,1,0:T(8,128)(2,1)} %bases_hbm.1, bf16[2,7,3,128,128]{4,3,2,1,0:T(8,128)(2,1)} %local_hbm.1, bf16[2,1,3,3,128,128]{5,4,3,2,1,0:T(8,128)(2,1)} %upper_hbm.1, ...), custom_call_target="tpu_custom_call" | custom-call | tf_op jit(solution)/shard_map/pallas_call | solution.py:815
  77.2 1.0 %copy.10 = f32[2048,128]{1,0:T(8,128)} copy(f32[2048,128]{1,0:T(8,128)S(1)} %bitcast.2) | data formatting | bytes 2097152
  78.1 0.6 copy.11

commit v4 on v3

--- a/solution.py
+++ b/solution.py
@@ -691,16 +691,14 @@
             square = jnp.sum((out * out).reshape(-1, 8, columns), axis=0)
             sums = square if sums is None else sums + square
         nrm[pl.ds(k, 1)] = jnp.sum(sums, axis=0, keepdims=True)
-        if k == STEPS - 1:
-            start_norms()
+        pl.when(k == STEPS - 1)(start_norms)
         beta = field_b[...] + combine(dot_nt(fall_b[...], flat))
         beta = beta + combine(dot(tree[1], stack[0]))
         for i in range(leaves):
             far = beta[i * rank : (i + 1) * rank].astype(BF16)
             value = x_ref[i] + (dot(near[1, i], rb[i]) + dot(bases[1, i, 0], far))
             x_ref[i] = value
-            if k < STEPS - 1:
-                xw[i] = wide(value)
+            xw[i] = wide(value)
         for copy in started:
             copy.wait_send()
 
@@ -788,8 +786,12 @@
 
     apply_first(prepare, [first, second, third, fourth, fifth])
     merged(0, [sixth, setup_fall, eighth])
-    for k in range(1, STEPS):
-        merged(k, [lambda: None])
+
+    def step(k, carry):
+        merged(k, [])
+        return carry
+
+    lax.fori_loop(1, STEPS, step, 0)
     finish_norms()
 
 

time: 78.9 us -> 79.6 us (level)
  Pallas kernels: 76.5 us -> 77.3 us
where the time goes in v4:
time: 79.6 us; the launch traced here: 79.5 us
  Pallas kernels  77.3 us (97%)
  local copies, waits for them, and re-layouts  1.55 us (2%)
    pallas_call x1, Pallas kernels, body(): pl.pallas_call(functools.partial(kernel, bits_leaf, bits_rows), out_shape...  77.3 us

profile of v4, /device:TPU:0, one launch (start us, length us, event | category | flops | bytes accessed | tf_op | source)
XLA Modules:
  0.0 79.5 jit_solution(4774733191794561155)
XLA Ops:
  0.6 77.3 %shard_map.77 = (f32[4,512,128]{2,1,0:T(8,128)S(1)}, f32[3,128]{1,0:T(4,128)S(1)}) custom-call(f32[4,512,128]{2,1,0:T(8,128)} %bitcast.3, bf16[2,4,512,512]{3,2,1,0:T(8,128)(2,1)} %near_hbm.1, bf16[2,4,2,512,128]{4,3,2,1,0:T(8,128)(2,1)} %bases_hbm.1, bf16[2,7,3,128,128]{4,3,2,1,0:T(8,128)(2,1)} %local_hbm.1, bf16[2,1,3,3,128,128]{5,4,3,2,1,0:T(8,128)(2,1)} %upper_hbm.1, ...), custom_call_target="tpu_custom_call" | custom-call | tf_op jit(solution)/shard_map/pallas_call | solution.py:817
  77.9 1.0 %copy.10 = f32[2048,128]{1,0:T(8,128)} copy(f32[2048,128]{1,0:T(8,128)S(1)} %bitcast.2) | data formatting | bytes 2097152
  78.9 0.6 copy.11
